TPU v7x, 128 devices: a whole 4x4x4 slice. The times are simulated.
128 devices in a mesh: rows: 16 (over y, x), tp: 8 (over z, core).
Axes of the slice: x: 4, y: 4, z: 4, core: 2. Of those that a mesh axis runs over, the one named last changes fastest.
Arguments:
- train_up: bfloat16 [5120, 20480], P('rows', 'tp'), may hold values from -0.078125 to 0.078125
- low_up: bfloat16 [5120, 16], P('rows'), may hold values from -0.078125 to 0.078125
- high_up: bfloat16 [16, 20480], P(None, 'tp'), may hold values from -1.5 to 1.5
- norm_train: float32 [5120], P(('rows', 'tp')), may hold values from 0.25 to 1.75
- norm_step: float32 [5120], P(('rows', 'tp')), may hold values from -0.3 to 0.3
Outputs:
- ready_up: bfloat16 [20480, 5120], P('tp')
- serve_norm: bfloat16 [5120], replicated
All inputs are finite; a program needn't handle non-finite values.
Results may differ from a plain program's by a relative error of at most 0.001.
Values may be sent and summed in bfloat16 or wider, within the bound.
A program may use at most 128 MiB of HBM per device.

v0:
```python
import jax
import jax.numpy as jnp
from jax import lax
from jax.sharding import PartitionSpec as P

mix_rate = 2.0


def per_device(train_up, low_up, high_up, norm_train, norm_step):
    latest_up = train_up.astype(jnp.float32) + mix_rate * jnp.dot(
        low_up, high_up, preferred_element_type=jnp.float32
    )
    narrow_up = latest_up.astype(jnp.bfloat16)
    ready_up = lax.all_gather(narrow_up, "rows", axis=0, tiled=True)
    ready_up = ready_up.T
    serve_norm = lax.all_gather(
        (norm_train + norm_step).astype(jnp.bfloat16), ("rows", "tp"), axis=0, tiled=True
    )
    return (ready_up, serve_norm)


def solution(mesh):
    placed = (P("rows", "tp"), P("rows", None), P(None, "tp"), P(("rows", "tp")), P(("rows", "tp")))
    return jax.shard_map(
        per_device, mesh=mesh, in_specs=placed, out_specs=(P("tp", None), P()), check_vma=False
    )
```

profile of v0, /device:TPU:1, one launch (start us, length us, event | category | flops | bytes accessed | tf_op | source)
XLA Modules:
  0.0 216.7 jit_solution(54756600640375317)
XLA Ops:
  7.2 0.0 copy-start
  7.2 0.0 copy-start.1
  7.2 0.0 copy-start.2
  7.2 0.0 all-gather.2.cloned.1.call-start
  7.2 0.8 copy-done
  8.1 3.2 %fusion.1 = bf16[320,2560]{1,0:T(8,128)(2,1)} fusion(bf16[320,16]{0,1:T(8,128)(2,1)} %param.6, bf16[16,2560]{1,0:T(8,128)(2,1)S(1)} %copy-done, bf16[320,2560]{1,0:T(8,128)(2,1)} %param.5), kind=kOutput, calls=%fused_computation.2 | convolution fusion | flops 29491200 | bytes 3368960 | tf_op jit(solution)/shard_map/dot_general | solution.py:10
  11.3 0.0 all-gather.2.cloned.1.call-update
  11.3 0.0 copy-done.1
  11.3 0.0 copy-done.2
  11.4 0.2 dynamic-update-slice
  11.6 72.0 %all-reduce = bf16[5120]{0:T(1024)(128)(2,1)} all-reduce(bf16[5120]{0:T(1024)(128)(2,1)S(1)} %dynamic-update-slice), channel_id=1, replica_groups=mesh['rows'=16,'tp'=8] {'rows','tp'}, use_global_device_ids=true, to_apply=%add | all-reduce | flops 5120 | bytes 20480
  83.6 91.2 %all-gather.2.cloned.1.call-done = bf16[5120,2560]{1,0:T(8,128)(2,1)} async-done(((bf16[320,2560]{1,0:T(8,128)(2,1)}), bf16[5120,2560]{1,0:T(8,128)(2,1)}) %all-gather.2.cloned.1.call-update) | async-done | bytes 26214416 | tf_op jit(solution)/shard_map/all_gather | solution.py:14
  174.8 35.1 %copy.7 = bf16[2560,5120]{1,0:T(8,128)(2,1)} copy(bf16[2560,5120]{0,1:T(8,128)(2,1)} %bitcast.3) | data formatting | bytes 52428800
  (2 shorter events, 0.0 us)
Async XLA Ops:
  7.2 0.9 copy-start
  7.2 4.1 %copy-start.1 = (f32[40]{0:T(128)S(1)}, f32[40]{0:T(128)}, u32[]{:S(2)}) copy-start(f32[40]{0:T(128)} %param.8) | copy-start | bytes 484
  7.2 4.1 %copy-start.2 = (f32[40]{0:T(128)S(1)}, f32[40]{0:T(128)}, u32[]{:S(2)}) copy-start(f32[40]{0:T(128)} %param.9) | copy-start | bytes 484
  7.2 167.6 %all-gather.2.cloned.1.call-start = ((), (), s32[]{:S(2)}) async-start(), calls=%async_computation | async-start | bytes 27852800 | tf_op jit(solution)/shard_map/all_gather | solution.py:14
Sparse Core Ops, SparseCore 0:
  11.4 163.3 all-gather.1
where the time goes:
time: 218 us; the launch traced here: 217 us
  waiting for transfers between devices  91.3 us (42%)
  blocking collectives  72 us (33%)
  local copies, waits for them, and re-layouts  36.1 us (17%)
  between operations  14.1 us (6%)
  matrix products  3.22 us (1%)
    all_gather x1, waiting for transfers between devices, per_device(): ready_up = lax.all_gather(narrow_up, 'rows', axis=0, tiled=True)  91.2 us
    unnamed x1, blocking collectives  72 us
    unnamed x9, local copies, waits for them, and re-layouts  36.1 us
  transfers between devices with their start and end apart: 1, of which 1 were waited for; matrix products, arithmetic and copies ran while one was open for 0% of the time, Pallas kernels for 0%

commit v1 on v0

v1 whole, which is shorter than its diff:
```python
import functools

import jax
import jax.numpy as jnp
from jax import lax
from jax.experimental import pallas as pl
from jax.experimental.pallas import tpu as pltpu
from jax.sharding import PartitionSpec as P

mix_rate = 2.0
MESH = pl.DeviceIdType.MESH
SIDE = 4
LANES = 128


def ring_position(cycle, device):
    y, x = device // SIDE, device % SIDE
    return SIDE * (y if cycle == 0 else x) + (x + y) % SIDE


def ring_device(cycle, position):
    a = position // SIDE
    b = (position % SIDE + SIDE - a) % SIDE
    return SIDE * a + b if cycle == 0 else SIDE * b + a


def kernel(
    n_rows, n_tp, depth, chunks, per_ring,
    train_ref, low_ref, high_ref, normt_ref, norms_ref,
    out_ref, norm_out_ref,
    train_buf, held, norm_all,
    load_sem, send_sem, recv_sem, norm_send1, norm_recv1, norm_send2, norm_recv2,
):
    me = lax.axis_index("rows")
    my_tp = lax.axis_index("tp")
    steps = n_rows - 1

    loads = []
    for c in range(chunks):
        load = pltpu.make_async_copy(train_ref.at[:, pl.ds(c * LANES, LANES)], train_buf.at[c], load_sem.at[c])
        loads.append(load)
    order = [q * per_ring + k for k in range(per_ring) for q in range(4)]
    for c in order:
        loads[c].start()

    barrier = pltpu.get_barrier_semaphore()
    for d in range(1, n_rows):
        pl.semaphore_signal(barrier, inc=1, device_id=((me + d) % n_rows, my_tp), device_id_type=MESH)
    for d in range(1, n_tp):
        pl.semaphore_signal(barrier, inc=1, device_id=(me, (my_tp + d) % n_tp), device_id_type=MESH)
    pl.semaphore_wait(barrier, n_rows + n_tp - 2)

    def ring_copy(c, origin, to, hop):
        q = c // per_ring
        rows = pl.ds(pl.multiple_of(origin * depth, 64), depth)
        return pltpu.make_async_remote_copy(
            src_ref=held.at[c, rows, :],
            dst_ref=held.at[c, rows, :],
            send_sem=send_sem.at[c],
            recv_sem=recv_sem.at[hop, c],
            device_id=(to, my_tp),
            device_id_type=MESH,
        )

    pos = [ring_position(q // 2, me) for q in range(4)]
    way = [1 if q % 2 == 0 else n_rows - 1 for q in range(4)]
    after = [ring_device(q // 2, (pos[q] + way[q]) % n_rows) for q in range(4)]

    def turn(c, origin):
        pair, odd = origin // 2, origin % 2
        base = pl.multiple_of(pair * 2 * depth, LANES)
        top = pl.multiple_of(origin * depth, 64)
        main = held[c, pl.ds(pl.multiple_of(top + odd * 64, 64), 256), :]
        out_ref[pl.ds(c * LANES, LANES), pl.ds(pl.multiple_of(base + odd * 384, LANES), 256)] = main.T
        rest = held[c, pl.ds(pl.multiple_of(top + (1 - odd) * 256, 64), 64), :]
        rest = jnp.concatenate([rest, rest], axis=0).T
        shared = out_ref.at[pl.ds(c * LANES, LANES), pl.ds(pl.multiple_of(base + 256, LANES), LANES)]

        @pl.when(odd == 0)
        def _():
            shared[:, :64] = rest[:, :64]

        @pl.when(odd == 1)
        def _():
            shared[:, 64:] = rest[:, 64:]

    low = low_ref[...].T
    mine = pl.ds(pl.multiple_of(me * depth, 64), depth)
    before = None
    for c in order:
        delta = jnp.dot(low, high_ref[:, c * LANES:(c + 1) * LANES], preferred_element_type=jnp.float32)
        loads[c].wait()
        held[c, mine, :] = (train_buf[c].astype(jnp.float32) + mix_rate * delta).astype(jnp.bfloat16)
        if before is not None:
            ring_copy(before, me, after[before // per_ring], 0).start()
        before = c
    slot = me * n_tp + my_tp
    norm_all[slot, :, :] = jnp.zeros((1, LANES), jnp.float32)
    norm_all[slot, :, 0:normt_ref.shape[1]] = normt_ref[...] + norms_ref[...]
    ring_copy(before, me, after[before // per_ring], 0).start()

    for c in order:
        turn(c, me)

    def norm_copy1(d):
        return pltpu.make_async_remote_copy(
            src_ref=norm_all.at[slot], dst_ref=norm_all.at[slot],
            send_sem=norm_send1.at[d], recv_sem=norm_recv1.at[d],
            device_id=(me, (my_tp + d) % n_tp), device_id_type=MESH)

    def norm_copy2(d):
        group = pl.ds(me * n_tp, n_tp)
        return pltpu.make_async_remote_copy(
            src_ref=norm_all.at[group], dst_ref=norm_all.at[group],
            send_sem=norm_send2.at[d], recv_sem=norm_recv2.at[d],
            device_id=((me + d) % n_rows, my_tp), device_id_type=MESH)

    for d in range(1, n_tp):
        norm_copy1(d).start()

    def arrived(hop, forward):
        for c in order:
            q = c // per_ring
            origin = ring_device(q // 2, (pos[q] + (n_rows - way[q]) * hop) % n_rows)
            ring_copy(c, origin, after[q], hop - 1).wait_recv()
            ring_copy(c, me, after[q], 0).wait_send()
            if forward:
                ring_copy(c, origin, after[q], hop).start()
            turn(c, origin)

    arrived(1, True)
    for d in range(1, n_tp):
        norm_copy1(d).wait()
    for d in range(1, n_rows):
        norm_copy2(d).start()
    lax.fori_loop(2, steps, lambda hop, _: (arrived(hop, True), _)[1], 0)
    for d in range(1, n_rows):
        norm_copy2(d).wait()
    width = normt_ref.shape[1]
    parts = [jnp.zeros((8, LANES), jnp.float32) for _ in range(6)]
    spot = lax.broadcasted_iota(jnp.int32, (8, LANES), 1)
    for i in range(16):
        row, shift = divmod(i * width, LANES)
        x = jnp.concatenate([norm_all[16 * g + i] for g in range(8)], axis=0)
        x = pltpu.roll(x, shift, 1) if shift else x
        first = (spot >= shift) & (spot < shift + width)
        parts[row] = jnp.where(first, x, parts[row])
        if shift + width > LANES:
            parts[row + 1] = jnp.where(spot < shift + width - LANES, x, parts[row + 1])
    for g in range(8):
        for row in range(5):
            norm_out_ref[5 * g + row : 5 * g + row + 1, :] = parts[row][g : g + 1, :]
    arrived(steps, False)


def write_kernel(pieces, held_ref, norm_ref, out_ref, norm_out_ref, sems):
    rows = held_ref.shape[0] // pieces
    copies = []
    for i in range(pieces):
        part = pl.ds(i * rows, rows)
        copies.append(pltpu.make_async_copy(held_ref.at[part, :], out_ref.at[part, :], sems.at[i]))
        copies[-1].start()
    norm_out_ref[...] = norm_ref[...]
    for copy in copies:
        copy.wait()


def per_device(train_up, low_up, high_up, norm_train, norm_step):
    n_rows, n_tp = lax.axis_size("rows"), lax.axis_size("tp")
    depth, width = train_up.shape
    chunks = width // LANES
    per_ring = chunks // 4
    ready, norm = pl.pallas_call(
        functools.partial(kernel, n_rows, n_tp, depth, chunks, per_ring),
        out_shape=(
            pltpu.VMEM((width, n_rows * depth), jnp.bfloat16),
            jax.ShapeDtypeStruct((n_rows * n_tp * norm_train.shape[0] // LANES, LANES), jnp.float32),
        ),
        in_specs=[pl.BlockSpec(memory_space=pl.ANY)] + [pl.BlockSpec(memory_space=pltpu.VMEM)] * 4,
        out_specs=(pl.BlockSpec(memory_space=pltpu.VMEM), pl.BlockSpec(memory_space=pltpu.VMEM)),
        scratch_shapes=[
            pltpu.VMEM((chunks, depth, LANES), jnp.bfloat16),
            pltpu.VMEM((chunks, n_rows * depth, LANES), jnp.bfloat16),
            pltpu.VMEM((n_rows * n_tp, 1, LANES), jnp.float32),
            pltpu.SemaphoreType.DMA((chunks,)),
            pltpu.SemaphoreType.DMA((chunks,)),
            pltpu.SemaphoreType.DMA((n_rows - 1, chunks)),
            pltpu.SemaphoreType.DMA((n_tp,)),
            pltpu.SemaphoreType.DMA((n_tp,)),
            pltpu.SemaphoreType.DMA((n_rows,)),
            pltpu.SemaphoreType.DMA((n_rows,)),
        ],
        compiler_params=pltpu.CompilerParams(
            collective_id=0, has_side_effects=True, vmem_limit_bytes=30*1024*1024
        ),
    )(train_up, low_up.T, high_up, norm_train.reshape(1, -1), norm_step.reshape(1, -1))
    ready, norm = pl.pallas_call(
        functools.partial(write_kernel, 16),
        out_shape=(
            jax.ShapeDtypeStruct(ready.shape, ready.dtype),
            jax.ShapeDtypeStruct(norm.shape, norm.dtype),
        ),
        in_specs=[pl.BlockSpec(memory_space=pl.ANY), pl.BlockSpec(memory_space=pltpu.VMEM)],
        out_specs=(pl.BlockSpec(memory_space=pl.ANY), pl.BlockSpec(memory_space=pltpu.VMEM)),
        scratch_shapes=[pltpu.SemaphoreType.DMA((16,))],
        compiler_params=pltpu.CompilerParams(vmem_limit_bytes=1024 * 1024),
    )(ready, norm)
    return ready, norm.reshape(-1).astype(jnp.bfloat16)


def solution(mesh):
    placed = (P("rows", "tp"), P("rows", None), P(None, "tp"), P(("rows", "tp")), P(("rows", "tp")))
    return jax.shard_map(
        per_device, mesh=mesh, in_specs=placed, out_specs=(P("tp", None), P()), check_vma=False
    )
```

time: 218 us -> 158 us (0.72)
  Pallas kernels: 0 us -> 156 us
  waiting for transfers between devices: 91.3 us -> 0 us
  blocking collectives: 72 us -> 0 us
  local copies, waits for them, and re-layouts: 36.1 us -> 0.72 us
  between operations: 14.1 us -> 0.66 us
  matrix products: 3.22 us -> 0 us
    pallas_call x0 -> x2, Pallas kernels: none -> 156 us  [the longest x1 147 us: per_device(): pl.pallas_call(functools.partial(kernel, n_rows, n_tp, depth, chunks, per...]
    all_gather x1 -> x0, waiting for transfers between devices: 91.2 us -> none  [per_device(): ready_up = lax.all_gather(narrow_up, 'rows', axis=0, tiled=True)]
    unnamed x1 -> x0, blocking collectives: 72 us -> none
    unnamed x9 -> x2, local copies, waits for them, and re-layouts: 36.1 us -> 0.72 us
    dot_general x1 -> x0, matrix products: 3.22 us -> none  [per_device(): jnp.dot(low_up, high_up, preferred_element_type=jnp.float32)]
  transfers between devices with their start and end apart: 1 -> 0, of which waited for: 1 -> 0; matrix products, arithmetic and copies ran while one was open for 0% -> 0% of each run, Pallas kernels for 0% -> 0%
where the time goes in v1:
time: 158 us
  Pallas kernels  156 us (99%)
    pallas_call x1, Pallas kernels, per_device(): pl.pallas_call(functools.partial(kernel, n_rows, n_tp, depth, chunks, per...  147 us
    pallas_call x1, Pallas kernels, per_device(): pl.pallas_call(functools.partial(write_kernel, 16), out_shape=(jax.ShapeD...  8.83 us

profile of v1, /device:TPU:1, one launch (start us, length us, event | category | flops | bytes accessed | tf_op | source)
XLA Modules:
  0.0 157.8 jit_solution(15471497997716239972)
XLA Ops:
  0.6 146.9 %shard_map.68 = (bf16[2560,5120]{1,0:T(8,128)(2,1)S(1)}, f32[40,128]{1,0:T(8,128)}) custom-call(bf16[320,2560]{1,0:T(8,128)(2,1)} %train_ref.1, bf16[16,320]{1,0:T(8,128)(2,1)} %bitcast.5, bf16[16,2560]{1,0:T(8,128)(2,1)} %high_ref.1, f32[1,40]{1,0:T(1,128)} %bitcast.6, f32[1,40]{1,0:T(1,128)} %bitcast.7), custom_call_target="tpu_custom_call" | custom-call | tf_op jit(solution)/shard_map/pallas_call | solution.py:173
  147.6 0.0 copy-start
  147.6 0.7 copy-done
  148.3 8.8 %shard_map.69 = (bf16[2560,5120]{1,0:T(8,128)(2,1)}, f32[40,128]{1,0:T(8,128)S(1)}) custom-call(bf16[2560,5120]{1,0:T(8,128)(2,1)S(1)} %get-tuple-element.6.held_ref, f32[40,128]{1,0:T(8,128)S(1)} %copy-done), custom_call_target="tpu_custom_call" | custom-call | tf_op jit(solution)/shard_map/pallas_call | solution.py:197
  157.2 0.6 convert_bitcast_fusion
Async XLA Ops:
  147.6 0.7 copy-start

commit v2 on v1

v2 whole, which is shorter than its diff:
```python
import functools

import jax
import jax.numpy as jnp
from jax import lax
from jax.experimental import pallas as pl
from jax.experimental.pallas import tpu as pltpu
from jax.sharding import PartitionSpec as P

mix_rate = 2.0
MESH = pl.DeviceIdType.MESH
SIDE = 4
LANES = 128


def ring_position(cycle, device):
    y, x = device // SIDE, device % SIDE
    return SIDE * (y if cycle == 0 else x) + (x + y) % SIDE


def ring_device(cycle, position):
    a = position // SIDE
    b = (position % SIDE + SIDE - a) % SIDE
    return SIDE * a + b if cycle == 0 else SIDE * b + a


def kernel(
    n_rows, n_tp, depth, chunks, per_ring,
    train_ref, low_ref, high_ref, normt_ref, norms_ref,
    out_ref, norm_out_ref,
    train_buf, low_buf, high_buf, norm_buf, held, norm_all,
    small_sem, load_sem, send_sem, recv_sem, norm_send, norm_recv, turn_send, turn_recv,
):
    me = lax.axis_index("rows")
    my_tp = lax.axis_index("tp")
    steps = n_rows - 1
    pos = [ring_position(q // 2, me) for q in range(4)]
    way = [1 if q % 2 == 0 else n_rows - 1 for q in range(4)]
    after = [ring_device(q // 2, (pos[q] + way[q]) % n_rows) for q in range(4)]
    twin = my_tp + 1 - 2 * (my_tp % 2)
    up, down = (my_tp + 2) % n_tp, (my_tp + n_tp - 2) % n_tp

    barrier = pltpu.get_barrier_semaphore()
    for q in range(4):
        pl.semaphore_signal(barrier, inc=1, device_id=(after[q], my_tp), device_id_type=MESH)
    for other in (twin, up, down):
        pl.semaphore_signal(barrier, inc=1, device_id=(me, other), device_id_type=MESH)

    order = [q * per_ring + k for k in range(per_ring) for q in range(4)]
    small = [
        pltpu.make_async_copy(low_ref, low_buf, small_sem.at[0]),
        pltpu.make_async_copy(high_ref, high_buf, small_sem.at[1]),
        pltpu.make_async_copy(normt_ref, norm_buf.at[0], small_sem.at[2]),
        pltpu.make_async_copy(norms_ref, norm_buf.at[1], small_sem.at[3]),
    ]
    loads = [
        pltpu.make_async_copy(train_ref.at[:, pl.ds(c * LANES, LANES)], train_buf.at[c], load_sem.at[c])
        for c in range(chunks)
    ]
    for load in small:
        load.start()
    for c in order:
        loads[c].start()

    def ring_copy(c, origin, to, hop):
        rows = pl.ds(pl.multiple_of(origin * depth, 64), depth)
        return pltpu.make_async_remote_copy(
            src_ref=held.at[c, rows, :],
            dst_ref=held.at[c, rows, :],
            send_sem=send_sem.at[c],
            recv_sem=recv_sem.at[hop, c],
            device_id=(to, my_tp),
            device_id_type=MESH,
        )

    def turn(c, origin):
        pair, odd = origin // 2, origin % 2
        base = pl.multiple_of(pair * 2 * depth, LANES)
        top = pl.multiple_of(origin * depth, 64)
        main = held[c, pl.ds(pl.multiple_of(top + odd * 64, 64), 256), :]
        out_ref[pl.ds(c * LANES, LANES), pl.ds(pl.multiple_of(base + odd * 384, LANES), 256)] = main.T
        rest = held[c, pl.ds(pl.multiple_of(top + (1 - odd) * 256, 64), 64), :]
        rest = jnp.concatenate([rest, rest], axis=0).T
        shared = out_ref.at[pl.ds(c * LANES, LANES), pl.ds(pl.multiple_of(base + 256, LANES), LANES)]

        @pl.when(odd == 0)
        def _():
            shared[:, :64] = rest[:, :64]

        @pl.when(odd == 1)
        def _():
            shared[:, 64:] = rest[:, 64:]

    slot = me * n_tp + my_tp
    width = normt_ref.shape[1]

    def norm_copy(i, first, count, device):
        part = pl.ds(first, count)
        return pltpu.make_async_remote_copy(
            src_ref=norm_all.at[part], dst_ref=norm_all.at[part],
            send_sem=norm_send.at[i], recv_sem=norm_recv.at[i],
            device_id=device, device_id_type=MESH)

    def pair_of(tp):
        return me * n_tp + (tp // 2) * 2

    norm_twin = norm_copy(0, slot, 1, (me, twin))
    norm_up = norm_copy(1, pair_of(my_tp), 2, (me, up))
    norm_down = norm_copy(2, pair_of(my_tp), 2, (me, down))
    norm_far = norm_copy(3, pair_of(down), 2, (me, up))

    def norm_turn(q, hop):
        origin = ring_device(0, (pos[q] + (n_rows - way[q]) * (hop - 1)) % n_rows)
        part = pl.ds(origin * n_tp, n_tp)
        return pltpu.make_async_remote_copy(
            src_ref=norm_all.at[part], dst_ref=norm_all.at[part],
            send_sem=turn_send.at[q, hop - 1], recv_sem=turn_recv.at[q, hop - 1],
            device_id=(after[q], my_tp), device_id_type=MESH)

    reach = (n_rows // 2, (n_rows - 1) // 2)

    def norm_step(hop):
        @pl.when(hop == 1)
        def _():
            norm_twin.wait()
            norm_up.start()
            norm_down.start()

        @pl.when(hop == 2)
        def _():
            norm_up.wait()
            norm_down.wait()
            norm_far.start()

        @pl.when(hop == 3)
        def _():
            norm_far.wait()

        turn_hop = hop - 2
        for q in range(2):
            @pl.when((turn_hop > 1) & (turn_hop <= reach[q] + 1))
            def _():
                norm_turn(q, turn_hop - 1).wait()

            @pl.when((turn_hop > 0) & (turn_hop <= reach[q]))
            def _():
                norm_turn(q, turn_hop).start()

    small[0].wait()
    low = low_buf[...].T
    small[1].wait()
    pl.semaphore_wait(barrier, 7)

    mine = pl.ds(pl.multiple_of(me * depth, 64), depth)
    before = None
    for c in order:
        delta = jnp.dot(low, high_buf[:, c * LANES:(c + 1) * LANES], preferred_element_type=jnp.float32)
        loads[c].wait()
        held[c, mine, :] = (train_buf[c].astype(jnp.float32) + mix_rate * delta).astype(jnp.bfloat16)
        if before is not None:
            ring_copy(before, me, after[before // per_ring], 0).start()
        before = c
    small[2].wait()
    small[3].wait()
    norm_all[slot, :, :] = jnp.zeros((1, LANES), jnp.float32)
    norm_all[slot, :, 0:width] = norm_buf[0] + norm_buf[1]
    ring_copy(before, me, after[before // per_ring], 0).start()

    for c in order:
        turn(c, me)
    norm_twin.start()

    def arrived(hop, forward):
        for c in order:
            q = c // per_ring
            origin = ring_device(q // 2, (pos[q] + (n_rows - way[q]) * hop) % n_rows)
            ring_copy(c, origin, after[q], hop - 1).wait_recv()
            ring_copy(c, me, after[q], 0).wait_send()
            if forward:
                ring_copy(c, origin, after[q], hop).start()
            turn(c, origin)

    def body(hop, carry):
        arrived(hop, True)
        norm_step(hop)
        return carry

    lax.fori_loop(1, steps, body, 0)

    parts = [jnp.zeros((8, LANES), jnp.float32) for _ in range(6)]
    spot = lax.broadcasted_iota(jnp.int32, (8, LANES), 1)
    for i in range(16):
        row, shift = divmod(i * width, LANES)
        x = jnp.concatenate([norm_all[16 * g + i] for g in range(8)], axis=0)
        x = pltpu.roll(x, shift, 1) if shift else x
        first = (spot >= shift) & (spot < shift + width)
        parts[row] = jnp.where(first, x, parts[row])
        if shift + width > LANES:
            parts[row + 1] = jnp.where(spot < shift + width - LANES, x, parts[row + 1])
    for g in range(8):
        for row in range(5):
            norm_out_ref[5 * g + row : 5 * g + row + 1, :] = parts[row][g : g + 1, :]
    arrived(steps, False)


def write_kernel(pieces, held_ref, norm_ref, out_ref, norm_out_ref, norm_buf, sems):
    rows = held_ref.shape[0] // pieces
    copies = []
    for i in range(pieces):
        part = pl.ds(i * rows, rows)
        copies.append(pltpu.make_async_copy(held_ref.at[part, :], out_ref.at[part, :], sems.at[i]))
        copies[-1].start()
    norm_buf[...] = norm_ref[...].astype(jnp.bfloat16)
    copies.append(pltpu.make_async_copy(norm_buf, norm_out_ref, sems.at[pieces]))
    copies[-1].start()
    for copy in copies:
        copy.wait()


def per_device(train_up, low_up, high_up, norm_train, norm_step):
    n_rows, n_tp = lax.axis_size("rows"), lax.axis_size("tp")
    depth, width = train_up.shape
    rank, own = low_up.shape[1], norm_train.shape[0]
    chunks = width // LANES
    per_ring = chunks // 4
    norm_shape = (n_rows * n_tp * own // LANES, LANES)
    held, norm = pl.pallas_call(
        functools.partial(kernel, n_rows, n_tp, depth, chunks, per_ring),
        out_shape=(
            pltpu.VMEM((width, n_rows * depth), jnp.bfloat16),
            pltpu.VMEM(norm_shape, jnp.float32),
        ),
        in_specs=[pl.BlockSpec(memory_space=pl.ANY)] * 5,
        out_specs=(pl.BlockSpec(memory_space=pltpu.VMEM), pl.BlockSpec(memory_space=pltpu.VMEM)),
        scratch_shapes=[
            pltpu.VMEM((chunks, depth, LANES), jnp.bfloat16),
            pltpu.VMEM((rank, depth), jnp.bfloat16),
            pltpu.VMEM((rank, width), jnp.bfloat16),
            pltpu.VMEM((2, 1, own), jnp.float32),
            pltpu.VMEM((chunks, n_rows * depth, LANES), jnp.bfloat16),
            pltpu.VMEM((n_rows * n_tp, 1, LANES), jnp.float32),
            pltpu.SemaphoreType.DMA((4,)),
            pltpu.SemaphoreType.DMA((chunks,)),
            pltpu.SemaphoreType.DMA((chunks,)),
            pltpu.SemaphoreType.DMA((n_rows - 1, chunks)),
            pltpu.SemaphoreType.DMA((4,)),
            pltpu.SemaphoreType.DMA((4,)),
            pltpu.SemaphoreType.DMA((2, n_rows // 2)),
            pltpu.SemaphoreType.DMA((2, n_rows // 2)),
        ],
        compiler_params=pltpu.CompilerParams(
            collective_id=0, has_side_effects=True, vmem_limit_bytes=30 * 1024 * 1024
        ),
    )(train_up, low_up.T, high_up, norm_train.reshape(1, -1), norm_step.reshape(1, -1))
    pieces = 16
    ready, norm = pl.pallas_call(
        functools.partial(write_kernel, pieces),
        out_shape=(
            jax.ShapeDtypeStruct(held.shape, held.dtype),
            jax.ShapeDtypeStruct(norm_shape, jnp.bfloat16),
        ),
        in_specs=[pl.BlockSpec(memory_space=pl.ANY), pl.BlockSpec(memory_space=pltpu.VMEM)],
        out_specs=(pl.BlockSpec(memory_space=pl.ANY), pl.BlockSpec(memory_space=pl.ANY)),
        scratch_shapes=[pltpu.VMEM(norm_shape, jnp.bfloat16), pltpu.SemaphoreType.DMA((pieces + 1,))],
        compiler_params=pltpu.CompilerParams(vmem_limit_bytes=1024 * 1024),
    )(held, norm)
    return ready, norm.reshape(-1)


def solution(mesh):
    placed = (P("rows", "tp"), P("rows", None), P(None, "tp"), P(("rows", "tp")), P(("rows", "tp")))
    return jax.shard_map(
        per_device, mesh=mesh, in_specs=placed, out_specs=(P("tp", None), P()), check_vma=False
    )
```

time: 158 us -> 154 us (0.975)
  Pallas kernels: 156 us -> 153 us
    pallas_call x1, Pallas kernels: 147 us -> 144 us  [per_device(): pl.pallas_call(functools.partial(kernel, n_rows, n_tp, depth, chunks, per...]
where the time goes in v2:
time: 154 us
  Pallas kernels  153 us (99%)
    pallas_call x1, Pallas kernels, per_device(): pl.pallas_call(functools.partial(kernel, n_rows, n_tp, depth, chunks, per...  144 us
    pallas_call x1, Pallas kernels, per_device(): pl.pallas_call(functools.partial(write_kernel, pieces), out_shape=(jax.Sh...  8.85 us

profile of v2, /device:TPU:1, one launch (start us, length us, event | category | flops | bytes accessed | tf_op | source)
XLA Modules:
  0.0 153.6 jit_solution(665231826466566504)
XLA Ops:
  0.6 144.1 %shard_map.68 = (bf16[2560,5120]{1,0:T(8,128)(2,1)S(1)}, f32[40,128]{1,0:T(8,128)S(1)}) custom-call(bf16[320,2560]{1,0:T(8,128)(2,1)} %train_ref.1, bf16[16,320]{1,0:T(8,128)(2,1)} %bitcast.4, bf16[16,2560]{1,0:T(8,128)(2,1)} %high_ref.1, f32[1,40]{1,0:T(1,128)} %bitcast.5, f32[1,40]{1,0:T(1,128)} %bitcast.6), custom_call_target="tpu_custom_call" | custom-call | tf_op jit(solution)/shard_map/pallas_call | solution.py:227
  144.8 8.8 %shard_map.69 = (bf16[2560,5120]{1,0:T(8,128)(2,1)}, bf16[40,128]{1,0:T(8,128)(2,1)}) custom-call(bf16[2560,5120]{1,0:T(8,128)(2,1)S(1)} %get-tuple-element.6.held_ref, f32[40,128]{1,0:T(8,128)S(1)} %get-tuple-element.7.norm_ref), custom_call_target="tpu_custom_call" | custom-call | tf_op jit(solution)/shard_map/pallas_call | solution.py:256

commit v3 on v2

--- a/solution.py
+++ b/solution.py
@@ -203,6 +203,15 @@
     arrived(steps, False)
 
 
+def scoped_kernel(n_rows, n_tp, depth, chunks, per_ring, *refs):
+    sem = pltpu.SemaphoreType.DMA
+    pl.run_scoped(
+        functools.partial(kernel, n_rows, n_tp, depth, chunks, per_ring, *refs),
+        sem((4,)), sem((chunks,)), sem((chunks,)), sem((n_rows - 1, chunks)),
+        sem((4,)), sem((4,)), sem((2, n_rows // 2)), sem((2, n_rows // 2)),
+    )
+
+
 def write_kernel(pieces, held_ref, norm_ref, out_ref, norm_out_ref, norm_buf, sems):
     rows = held_ref.shape[0] // pieces
     copies = []
@@ -225,7 +234,7 @@
     per_ring = chunks // 4
     norm_shape = (n_rows * n_tp * own // LANES, LANES)
     held, norm = pl.pallas_call(
-        functools.partial(kernel, n_rows, n_tp, depth, chunks, per_ring),
+        functools.partial(scoped_kernel, n_rows, n_tp, depth, chunks, per_ring),
         out_shape=(
             pltpu.VMEM((width, n_rows * depth), jnp.bfloat16),
             pltpu.VMEM(norm_shape, jnp.float32),
@@ -239,14 +248,6 @@
             pltpu.VMEM((2, 1, own), jnp.float32),
             pltpu.VMEM((chunks, n_rows * depth, LANES), jnp.bfloat16),
             pltpu.VMEM((n_rows * n_tp, 1, LANES), jnp.float32),
-            pltpu.SemaphoreType.DMA((4,)),
-            pltpu.SemaphoreType.DMA((chunks,)),
-            pltpu.SemaphoreType.DMA((chunks,)),
-            pltpu.SemaphoreType.DMA((n_rows - 1, chunks)),
-            pltpu.SemaphoreType.DMA((4,)),
-            pltpu.SemaphoreType.DMA((4,)),
-            pltpu.SemaphoreType.DMA((2, n_rows // 2)),
-            pltpu.SemaphoreType.DMA((2, n_rows // 2)),
         ],
         compiler_params=pltpu.CompilerParams(
             collective_id=0, has_side_effects=True, vmem_limit_bytes=30 * 1024 * 1024

time: 154 us -> 150 us (0.974)
  Pallas kernels: 153 us -> 150 us
    pallas_call x1, Pallas kernels: 144 us -> 141 us  [per_device(): pl.pallas_call(functools.partial(scoped_kernel, n_rows, n_tp, depth, chun...]
where the time goes in v3:
time: 150 us
  Pallas kernels  150 us (100%)
    pallas_call x1, Pallas kernels, per_device(): pl.pallas_call(functools.partial(scoped_kernel, n_rows, n_tp, depth, chun...  141 us
    pallas_call x1, Pallas kernels, per_device(): pl.pallas_call(functools.partial(write_kernel, pieces), out_shape=(jax.Sh...  8.85 us

profile of v3, /device:TPU:1, one launch (start us, length us, event | category | flops | bytes accessed | tf_op | source)
XLA Modules:
  0.0 150.2 jit_solution(9183500640498615773)
XLA Ops:
  0.6 140.7 %shard_map.68 = (bf16[2560,5120]{1,0:T(8,128)(2,1)S(1)}, f32[40,128]{1,0:T(8,128)S(1)}) custom-call(bf16[320,2560]{1,0:T(8,128)(2,1)} %refs_0_.1, bf16[16,320]{1,0:T(8,128)(2,1)} %bitcast.4, bf16[16,2560]{1,0:T(8,128)(2,1)} %refs_2_.1, f32[1,40]{1,0:T(1,128)} %bitcast.5, f32[1,40]{1,0:T(1,128)} %bitcast.6), custom_call_target="tpu_custom_call" | custom-call | tf_op jit(solution)/shard_map/pallas_call | solution.py:236
  141.3 8.8 %shard_map.69 = (bf16[2560,5120]{1,0:T(8,128)(2,1)}, bf16[40,128]{1,0:T(8,128)(2,1)}) custom-call(bf16[2560,5120]{1,0:T(8,128)(2,1)S(1)} %get-tuple-element.6.held_ref, f32[40,128]{1,0:T(8,128)S(1)} %get-tuple-element.7.norm_ref), custom_call_target="tpu_custom_call" | custom-call | tf_op jit(solution)/shard_map/pallas_call | solution.py:257

commit v4 on v3

--- a/solution.py
+++ b/solution.py
@@ -9,6 +9,7 @@
 
 mix_rate = 2.0
 MESH = pl.DeviceIdType.MESH
+SPLIT = 3
 SIDE = 4
 LANES = 128
 
@@ -24,16 +25,30 @@
     return SIDE * a + b if cycle == 0 else SIDE * b + a
 
 
+def put_half(tile, value, half):
+    @pl.when(half == 0)
+    def _():
+        tile[:, :64] = value[:, :64]
+
+    @pl.when(half == 1)
+    def _():
+        tile[:, 64:] = value[:, 64:]
+
+
+def splits(tp):
+    return 1 - tp % 2
+
+
 def kernel(
     n_rows, n_tp, depth, chunks, per_ring,
     train_ref, low_ref, high_ref, normt_ref, norms_ref,
-    out_ref, norm_out_ref,
+    out_ref, mine_ref, norm_out_ref,
     train_buf, low_buf, high_buf, norm_buf, held, norm_all,
     small_sem, load_sem, send_sem, recv_sem, norm_send, norm_recv, turn_send, turn_recv,
 ):
     me = lax.axis_index("rows")
     my_tp = lax.axis_index("tp")
-    steps = n_rows - 1
+    steps = n_rows - 1 - SPLIT * splits(my_tp)
     pos = [ring_position(q // 2, me) for q in range(4)]
     way = [1 if q % 2 == 0 else n_rows - 1 for q in range(4)]
     after = [ring_device(q // 2, (pos[q] + way[q]) % n_rows) for q in range(4)]
@@ -62,10 +77,10 @@
     for c in order:
         loads[c].start()
 
-    def ring_copy(c, origin, to, hop):
+    def ring_copy(c, origin, to, hop, first=False):
         rows = pl.ds(pl.multiple_of(origin * depth, 64), depth)
         return pltpu.make_async_remote_copy(
-            src_ref=held.at[c, rows, :],
+            src_ref=mine_ref.at[c] if first else held.at[c, rows, :],
             dst_ref=held.at[c, rows, :],
             send_sem=send_sem.at[c],
             recv_sem=recv_sem.at[hop, c],
@@ -73,23 +88,17 @@
             device_id_type=MESH,
         )
 
-    def turn(c, origin):
+    def turn(c, origin, first=False):
         pair, odd = origin // 2, origin % 2
         base = pl.multiple_of(pair * 2 * depth, LANES)
-        top = pl.multiple_of(origin * depth, 64)
-        main = held[c, pl.ds(pl.multiple_of(top + odd * 64, 64), 256), :]
+        top = 0 if first else origin * depth
+        source = mine_ref if first else held
+        main = source[c, pl.ds(pl.multiple_of(top + odd * 64, 64), 256), :]
         out_ref[pl.ds(c * LANES, LANES), pl.ds(pl.multiple_of(base + odd * 384, LANES), 256)] = main.T
-        rest = held[c, pl.ds(pl.multiple_of(top + (1 - odd) * 256, 64), 64), :]
+        rest = source[c, pl.ds(pl.multiple_of(top + (1 - odd) * 256, 64), 64), :]
         rest = jnp.concatenate([rest, rest], axis=0).T
         shared = out_ref.at[pl.ds(c * LANES, LANES), pl.ds(pl.multiple_of(base + 256, LANES), LANES)]
-
-        @pl.when(odd == 0)
-        def _():
-            shared[:, :64] = rest[:, :64]
-
-        @pl.when(odd == 1)
-        def _():
-            shared[:, 64:] = rest[:, 64:]
+        put_half(shared, rest, odd)
 
     slot = me * n_tp + my_tp
     width = normt_ref.shape[1]
@@ -151,23 +160,22 @@
     small[1].wait()
     pl.semaphore_wait(barrier, 7)
 
-    mine = pl.ds(pl.multiple_of(me * depth, 64), depth)
     before = None
     for c in order:
         delta = jnp.dot(low, high_buf[:, c * LANES:(c + 1) * LANES], preferred_element_type=jnp.float32)
         loads[c].wait()
-        held[c, mine, :] = (train_buf[c].astype(jnp.float32) + mix_rate * delta).astype(jnp.bfloat16)
+        mine_ref[c] = (train_buf[c].astype(jnp.float32) + mix_rate * delta).astype(jnp.bfloat16)
         if before is not None:
-            ring_copy(before, me, after[before // per_ring], 0).start()
+            ring_copy(before, me, after[before // per_ring], 0, True).start()
         before = c
     small[2].wait()
     small[3].wait()
     norm_all[slot, :, :] = jnp.zeros((1, LANES), jnp.float32)
     norm_all[slot, :, 0:width] = norm_buf[0] + norm_buf[1]
-    ring_copy(before, me, after[before // per_ring], 0).start()
+    ring_copy(before, me, after[before // per_ring], 0, True).start()
 
     for c in order:
-        turn(c, me)
+        turn(c, me, True)
     norm_twin.start()
 
     def arrived(hop, forward):
@@ -175,7 +183,7 @@
             q = c // per_ring
             origin = ring_device(q // 2, (pos[q] + (n_rows - way[q]) * hop) % n_rows)
             ring_copy(c, origin, after[q], hop - 1).wait_recv()
-            ring_copy(c, me, after[q], 0).wait_send()
+            ring_copy(c, me, after[q], 0, True).wait_send()
             if forward:
                 ring_copy(c, origin, after[q], hop).start()
             turn(c, origin)
@@ -212,6 +220,90 @@
     )
 
 
+def late_place(n_rows, q, me, away):
+    position, way = ring_position(q // 2, me), 1 if q % 2 == 0 else n_rows - 1
+    origin = ring_device(q // 2, (position + way * away) % n_rows)
+    other = origin + 1 - 2 * (origin % 2)
+    gap = (ring_position(q // 2, other) + n_rows - position) * way % n_rows
+    return origin, gap
+
+
+def late_kernel(
+    n_rows, depth, chunks, per_ring, first_ref, mine_ref, patch_ref, late, stash, send_sem, recv_sem, stash_sem
+):
+    me = lax.axis_index("rows")
+    my_tp = lax.axis_index("tp")
+    order = [q * per_ring + k for k in range(per_ring) for q in range(4)]
+
+    def neighbour(q, step):
+        way = 1 if q % 2 == 0 else n_rows - 1
+        return ring_device(q // 2, (ring_position(q // 2, me) + step * way) % n_rows)
+
+    def late_copy(c, hop, first):
+        q = c // per_ring
+        return pltpu.make_async_remote_copy(
+            src_ref=mine_ref.at[c] if first else late.at[hop - 1, c],
+            dst_ref=late.at[hop, c],
+            send_sem=send_sem.at[c],
+            recv_sem=recv_sem.at[hop, c],
+            device_id=(neighbour(q, n_rows - 1), my_tp),
+            device_id_type=MESH,
+        )
+
+    def stash_copy(q, slot):
+        origin, _ = late_place(n_rows, q, me, slot + 1)
+        rows = pl.ds(q * per_ring * LANES, per_ring * LANES)
+        lanes = pl.ds(pl.multiple_of(origin // 2 * 2 * depth + 256, LANES), LANES)
+        return pltpu.make_async_copy(first_ref.at[rows, lanes], stash.at[slot, rows, :], stash_sem.at[slot, q])
+
+    def turn(c, slot):
+        q = c // per_ring
+        origin, gap = late_place(n_rows, q, me, slot + 1)
+        odd = origin % 2
+        rows = pl.ds(c * LANES, LANES)
+        main = late[slot, c, pl.ds(pl.multiple_of(odd * 64, 64), 256), :]
+        patch_ref[slot, rows, 0:256] = main.T
+        rest = late[slot, c, pl.ds(pl.multiple_of((1 - odd) * 256, 64), 64), :]
+        shared = patch_ref.at[slot, rows, 256:384]
+        put_half(shared, jnp.concatenate([rest, rest], axis=0).T, odd)
+
+        @pl.when((gap == 0) | (gap > SPLIT))
+        def _():
+            put_half(shared, stash[slot, rows, :], 1 - odd)
+
+        @pl.when((gap > 0) & (gap <= slot))
+        def _():
+            put_half(shared, patch_ref[gap - 1, rows, 256:384], 1 - odd)
+
+    @pl.when(splits(my_tp) == 1)
+    def _():
+        barrier = pltpu.get_barrier_semaphore()
+        for q in range(4):
+            pl.semaphore_signal(barrier, inc=1, device_id=(neighbour(q, 1), my_tp), device_id_type=MESH)
+        pl.semaphore_wait(barrier, 4)
+        for c in order:
+            late_copy(c, 0, True).start()
+        stashed = [stash_copy(q, slot) for slot in range(SPLIT) for q in range(4)]
+        for copy in stashed:
+            copy.start()
+        for copy in stashed:
+            copy.wait()
+        for hop in range(SPLIT):
+            for c in order:
+                late_copy(c, hop, hop == 0).wait()
+                if hop + 1 < SPLIT:
+                    late_copy(c, hop + 1, False).start()
+                turn(c, hop)
+
+
+def scoped_late_kernel(n_rows, depth, chunks, per_ring, *refs):
+    sem = pltpu.SemaphoreType.DMA
+    pl.run_scoped(
+        functools.partial(late_kernel, n_rows, depth, chunks, per_ring, *refs),
+        sem((chunks,)), sem((SPLIT, chunks)), sem((SPLIT, 4)),
+    )
+
+
 def write_kernel(pieces, held_ref, norm_ref, out_ref, norm_out_ref, norm_buf, sems):
     rows = held_ref.shape[0] // pieces
     copies = []
@@ -226,6 +318,31 @@
         copy.wait()
 
 
+def patch_kernel(n_rows, depth, quarter, patch_ref, first_ref, out_ref, main_sem, shared_sem):
+    me = lax.axis_index("rows")
+
+    def copies(q, slot):
+        origin, gap = late_place(n_rows, q, me, slot + 1)
+        base = origin // 2 * 2 * depth
+        rows = pl.ds(q * quarter, quarter)
+        lanes = pl.ds(pl.multiple_of(base + origin % 2 * 384, LANES), 256)
+        shared_lanes = pl.ds(pl.multiple_of(base + 256, LANES), LANES)
+        main = pltpu.make_async_copy(patch_ref.at[slot, rows, 0:256], out_ref.at[rows, lanes], main_sem.at[slot, q])
+        shared = pltpu.make_async_copy(
+            patch_ref.at[slot, rows, 256:384], out_ref.at[rows, shared_lanes], shared_sem.at[slot, q])
+        return main, shared, (gap <= slot) | (gap > SPLIT)
+
+    @pl.when(splits(lax.axis_index("tp")) == 1)
+    def _():
+        everything = [copies(q, slot) for slot in range(SPLIT) for q in range(4)]
+        for main, shared, last in everything:
+            main.start()
+            pl.when(last)(shared.start)
+        for main, shared, last in everything:
+            main.wait()
+            pl.when(last)(shared.wait)
+
+
 def per_device(train_up, low_up, high_up, norm_train, norm_step):
     n_rows, n_tp = lax.axis_size("rows"), lax.axis_size("tp")
     depth, width = train_up.shape
@@ -233,14 +350,16 @@
     chunks = width // LANES
     per_ring = chunks // 4
     norm_shape = (n_rows * n_tp * own // LANES, LANES)
-    held, norm = pl.pallas_call(
+    anywhere, vmem = pl.BlockSpec(memory_space=pl.ANY), pl.BlockSpec(memory_space=pltpu.VMEM)
+    held, mine, norm = pl.pallas_call(
         functools.partial(scoped_kernel, n_rows, n_tp, depth, chunks, per_ring),
         out_shape=(
             pltpu.VMEM((width, n_rows * depth), jnp.bfloat16),
+            pltpu.VMEM((chunks, depth, LANES), jnp.bfloat16),
             pltpu.VMEM(norm_shape, jnp.float32),
         ),
-        in_specs=[pl.BlockSpec(memory_space=pl.ANY)] * 5,
-        out_specs=(pl.BlockSpec(memory_space=pltpu.VMEM), pl.BlockSpec(memory_space=pltpu.VMEM)),
+        in_specs=[anywhere] * 5,
+        out_specs=(vmem, vmem, vmem),
         scratch_shapes=[
             pltpu.VMEM((chunks, depth, LANES), jnp.bfloat16),
             pltpu.VMEM((rank, depth), jnp.bfloat16),
@@ -254,17 +373,39 @@
         ),
     )(train_up, low_up.T, high_up, norm_train.reshape(1, -1), norm_step.reshape(1, -1))
     pieces = 16
-    ready, norm = pl.pallas_call(
+    first, norm = pl.pallas_call(
         functools.partial(write_kernel, pieces),
         out_shape=(
             jax.ShapeDtypeStruct(held.shape, held.dtype),
             jax.ShapeDtypeStruct(norm_shape, jnp.bfloat16),
         ),
-        in_specs=[pl.BlockSpec(memory_space=pl.ANY), pl.BlockSpec(memory_space=pltpu.VMEM)],
-        out_specs=(pl.BlockSpec(memory_space=pl.ANY), pl.BlockSpec(memory_space=pl.ANY)),
+        in_specs=[anywhere, vmem],
+        out_specs=(anywhere, anywhere),
         scratch_shapes=[pltpu.VMEM(norm_shape, jnp.bfloat16), pltpu.SemaphoreType.DMA((pieces + 1,))],
         compiler_params=pltpu.CompilerParams(vmem_limit_bytes=1024 * 1024),
     )(held, norm)
+    patch = pl.pallas_call(
+        functools.partial(scoped_late_kernel, n_rows, depth, chunks, per_ring),
+        out_shape=pltpu.VMEM((SPLIT, width, 384), jnp.bfloat16),
+        in_specs=[anywhere, vmem],
+        out_specs=vmem,
+        scratch_shapes=[
+            pltpu.VMEM((SPLIT, chunks, depth, LANES), jnp.bfloat16),
+            pltpu.VMEM((SPLIT, width, LANES), jnp.bfloat16),
+        ],
+        compiler_params=pltpu.CompilerParams(
+            collective_id=1, has_side_effects=True, vmem_limit_bytes=40 * 1024 * 1024
+        ),
+    )(first, mine)
+    ready = pl.pallas_call(
+        functools.partial(patch_kernel, n_rows, depth, width // 4),
+        out_shape=jax.ShapeDtypeStruct(held.shape, held.dtype),
+        in_specs=[anywhere, anywhere],
+        out_specs=anywhere,
+        input_output_aliases={1: 0},
+        scratch_shapes=[pltpu.SemaphoreType.DMA((SPLIT, 4)), pltpu.SemaphoreType.DMA((SPLIT, 4))],
+        compiler_params=pltpu.CompilerParams(vmem_limit_bytes=1024 * 1024),
+    )(patch, first)
     return ready, norm.reshape(-1)
 
 

time: 150 us -> 147 us (0.980)
  the two profiles are of different devices: /device:TPU:1 before, /device:TPU:0 now
where the time goes in v4:
time: 147 us
  Pallas kernels  146 us (99%)
    pallas_call x1, Pallas kernels, per_device(): pl.pallas_call(functools.partial(scoped_kernel, n_rows, n_tp, depth, chun...  116 us
    pallas_call x1, Pallas kernels, per_device(): pl.pallas_call(functools.partial(scoped_late_kernel, n_rows, depth, chunk...  19.3 us
    pallas_call x1, Pallas kernels, per_device(): pl.pallas_call(functools.partial(write_kernel, pieces), out_shape=(jax.Sh...  8.85 us

profile of v4, /device:TPU:0, one launch (start us, length us, event | category | flops | bytes accessed | tf_op | source)
XLA Modules:
  0.0 147.1 jit_solution(6253585244329144068)
XLA Ops:
  0.6 115.6 %shard_map.68 = (bf16[2560,5120]{1,0:T(8,128)(2,1)S(1)}, bf16[20,320,128]{2,1,0:T(8,128)(2,1)S(1)}, f32[40,128]{1,0:T(8,128)S(1)}) custom-call(bf16[320,2560]{1,0:T(8,128)(2,1)} %refs_0_.1, bf16[16,320]{1,0:T(8,128)(2,1)} %bitcast.4, bf16[16,2560]{1,0:T(8,128)(2,1)} %refs_2_.1, f32[1,40]{1,0:T(1,128)} %bitcast.5, f32[1,40]{1,0:T(1,128)} %bitcast.6), custom_call_target="tpu_custom_call" | custom-call | tf_op jit(solution)/shard_map/pallas_call | solution.py:354
  116.3 8.8 %shard_map.69 = (bf16[2560,5120]{1,0:T(8,128)(2,1)}, bf16[40,128]{1,0:T(8,128)(2,1)}) custom-call(bf16[2560,5120]{1,0:T(8,128)(2,1)S(1)} %get-tuple-element.7.held_ref, f32[40,128]{1,0:T(8,128)S(1)} %get-tuple-element.8.norm_ref), custom_call_target="tpu_custom_call" | custom-call | tf_op jit(solution)/shard_map/pallas_call | solution.py:376
  125.1 19.3 %shard_map.70.patch_ref = bf16[3,2560,384]{2,1,0:T(8,128)(2,1)S(1)} custom-call(bf16[2560,5120]{1,0:T(8,128)(2,1)} %get-tuple-element.9.refs_0_.first_ref, bf16[20,320,128]{2,1,0:T(8,128)(2,1)S(1)} %get-tuple-element.10.refs_1_), custom_call_target="tpu_custom_call" | custom-call | tf_op jit(solution)/shard_map/pallas_call | solution.py:387
  144.4 2.7 %shard_map.71 = bf16[2560,5120]{1,0:T(8,128)(2,1)} custom-call(bf16[3,2560,384]{2,1,0:T(8,128)(2,1)S(1)} %shard_map.70.patch_ref, bf16[2560,5120]{1,0:T(8,128)(2,1)} %get-tuple-element.9.refs_0_.first_ref), custom_call_target="tpu_custom_call", output_to_operand_aliasing={{}: (1, {})} | custom-call | tf_op jit(solution)/shard_map/pallas_call | solution.py:400

commit v5 on v4

--- a/solution.py
+++ b/solution.py
@@ -36,7 +36,7 @@
 
 
 def splits(tp):
-    return 1 - tp % 2
+    return tp % 2
 
 
 def kernel(
@@ -158,13 +158,13 @@
     small[0].wait()
     low = low_buf[...].T
     small[1].wait()
-    pl.semaphore_wait(barrier, 7)
-
     before = None
     for c in order:
         delta = jnp.dot(low, high_buf[:, c * LANES:(c + 1) * LANES], preferred_element_type=jnp.float32)
         loads[c].wait()
         mine_ref[c] = (train_buf[c].astype(jnp.float32) + mix_rate * delta).astype(jnp.bfloat16)
+        if c == order[1]:
+            pl.semaphore_wait(barrier, 7)
         if before is not None:
             ring_copy(before, me, after[before // per_ring], 0, True).start()
         before = c

time: 147 us -> 145 us (0.986)
  the two profiles are of different devices: /device:TPU:0 before, /device:TPU:1 now
where the time goes in v5:
time: 145 us
  Pallas kernels  145 us (100%)
    pallas_call x1, Pallas kernels, per_device(): pl.pallas_call(functools.partial(scoped_kernel, n_rows, n_tp, depth, chun...  114 us
    pallas_call x1, Pallas kernels, per_device(): pl.pallas_call(functools.partial(scoped_late_kernel, n_rows, depth, chunk...  19 us
    pallas_call x1, Pallas kernels, per_device(): pl.pallas_call(functools.partial(write_kernel, pieces), out_shape=(jax.Sh...  8.85 us

profile of v5, /device:TPU:1, one launch (start us, length us, event | category | flops | bytes accessed | tf_op | source)
XLA Modules:
  0.0 145.3 jit_solution(4004329665529039500)
XLA Ops:
  0.6 114.0 %shard_map.68 = (bf16[2560,5120]{1,0:T(8,128)(2,1)S(1)}, bf16[20,320,128]{2,1,0:T(8,128)(2,1)S(1)}, f32[40,128]{1,0:T(8,128)S(1)}) custom-call(bf16[320,2560]{1,0:T(8,128)(2,1)} %refs_0_.1, bf16[16,320]{1,0:T(8,128)(2,1)} %bitcast.4, bf16[16,2560]{1,0:T(8,128)(2,1)} %refs_2_.1, f32[1,40]{1,0:T(1,128)} %bitcast.5, f32[1,40]{1,0:T(1,128)} %bitcast.6), custom_call_target="tpu_custom_call" | custom-call | tf_op jit(solution)/shard_map/pallas_call | solution.py:354
  114.7 8.8 %shard_map.69 = (bf16[2560,5120]{1,0:T(8,128)(2,1)}, bf16[40,128]{1,0:T(8,128)(2,1)}) custom-call(bf16[2560,5120]{1,0:T(8,128)(2,1)S(1)} %get-tuple-element.7.held_ref, f32[40,128]{1,0:T(8,128)S(1)} %get-tuple-element.8.norm_ref), custom_call_target="tpu_custom_call" | custom-call | tf_op jit(solution)/shard_map/pallas_call | solution.py:376
  123.5 19.0 %shard_map.70.patch_ref = bf16[3,2560,384]{2,1,0:T(8,128)(2,1)S(1)} custom-call(bf16[2560,5120]{1,0:T(8,128)(2,1)} %get-tuple-element.9.refs_0_.first_ref, bf16[20,320,128]{2,1,0:T(8,128)(2,1)S(1)} %get-tuple-element.10.refs_1_), custom_call_target="tpu_custom_call" | custom-call | tf_op jit(solution)/shard_map/pallas_call | solution.py:387
  142.6 2.7 %shard_map.71 = bf16[2560,5120]{1,0:T(8,128)(2,1)} custom-call(bf16[3,2560,384]{2,1,0:T(8,128)(2,1)S(1)} %shard_map.70.patch_ref, bf16[2560,5120]{1,0:T(8,128)(2,1)} %get-tuple-element.9.refs_0_.first_ref), custom_call_target="tpu_custom_call", output_to_operand_aliasing={{}: (1, {})} | custom-call | tf_op jit(solution)/shard_map/pallas_call | solution.py:400

commit v6 on v5

--- a/solution.py
+++ b/solution.py
@@ -43,8 +43,8 @@
     n_rows, n_tp, depth, chunks, per_ring,
     train_ref, low_ref, high_ref, normt_ref, norms_ref,
     out_ref, mine_ref, norm_out_ref,
-    train_buf, low_buf, high_buf, norm_buf, held, norm_all,
-    small_sem, load_sem, send_sem, recv_sem, norm_send, norm_recv, turn_send, turn_recv,
+    train_buf, low_buf, high_buf, norm_buf, held, norm_all, norm_lines, norm_line,
+    small_sem, load_sem, send_sem, recv_sem, norm_send, norm_recv, turn_send, turn_recv, line_send, line_recv,
 ):
     me = lax.axis_index("rows")
     my_tp = lax.axis_index("tp")
@@ -58,8 +58,12 @@
     barrier = pltpu.get_barrier_semaphore()
     for q in range(4):
         pl.semaphore_signal(barrier, inc=1, device_id=(after[q], my_tp), device_id_type=MESH)
-    for other in (twin, up, down):
-        pl.semaphore_signal(barrier, inc=1, device_id=(me, other), device_id_type=MESH)
+    gateway = me == 0
+
+    @pl.when(gateway)
+    def _():
+        for other in (twin, up, down):
+            pl.semaphore_signal(barrier, inc=1, device_id=(me, other), device_id_type=MESH)
 
     order = [q * per_ring + k for k in range(per_ring) for q in range(4)]
     small = [
@@ -100,60 +104,92 @@
         shared = out_ref.at[pl.ds(c * LANES, LANES), pl.ds(pl.multiple_of(base + 256, LANES), LANES)]
         put_half(shared, rest, odd)
 
-    slot = me * n_tp + my_tp
+    slot = my_tp * n_rows + me
     width = normt_ref.shape[1]
 
-    def norm_copy(i, first, count, device):
-        part = pl.ds(first, count)
+    def norm_copy(i, first, count, other):
+        part = pl.ds(first * n_rows, count * n_rows)
         return pltpu.make_async_remote_copy(
             src_ref=norm_all.at[part], dst_ref=norm_all.at[part],
             send_sem=norm_send.at[i], recv_sem=norm_recv.at[i],
-            device_id=device, device_id_type=MESH)
-
-    def pair_of(tp):
-        return me * n_tp + (tp // 2) * 2
-
-    norm_twin = norm_copy(0, slot, 1, (me, twin))
-    norm_up = norm_copy(1, pair_of(my_tp), 2, (me, up))
-    norm_down = norm_copy(2, pair_of(my_tp), 2, (me, down))
-    norm_far = norm_copy(3, pair_of(down), 2, (me, up))
+            device_id=(me, other), device_id_type=MESH)
+
+    norm_twin = norm_copy(0, my_tp, 1, twin)
+    norm_up = norm_copy(1, my_tp // 2 * 2, 2, up)
+    norm_down = norm_copy(2, my_tp // 2 * 2, 2, down)
+    norm_far = norm_copy(3, down // 2 * 2, 2, up)
 
     def norm_turn(q, hop):
         origin = ring_device(0, (pos[q] + (n_rows - way[q]) * (hop - 1)) % n_rows)
-        part = pl.ds(origin * n_tp, n_tp)
+        part = pl.ds(my_tp * n_rows + origin, 1)
         return pltpu.make_async_remote_copy(
             src_ref=norm_all.at[part], dst_ref=norm_all.at[part],
             send_sem=turn_send.at[q, hop - 1], recv_sem=turn_recv.at[q, hop - 1],
             device_id=(after[q], my_tp), device_id_type=MESH)
 
+    def norm_pass(q):
+        return pltpu.make_async_remote_copy(
+            src_ref=norm_line, dst_ref=norm_line, send_sem=line_send.at[q], recv_sem=line_recv.at[q],
+            device_id=(after[q], my_tp), device_id_type=MESH)
+
     reach = (n_rows // 2, (n_rows - 1) // 2)
-
-    def norm_step(hop):
-        @pl.when(hop == 1)
+    far = (pos[0], (n_rows - pos[0]) % n_rows)
+    passes = [far[q] < reach[q] for q in range(2)]
+    takes = [(far[q] > 0) & (far[q] <= reach[q]) for q in range(2)]
+    meet = n_rows // 2
+
+    def assemble():
+        parts = [jnp.zeros((8, LANES), jnp.float32) for _ in range(6)]
+        spot = lax.broadcasted_iota(jnp.int32, (8, LANES), 1)
+        for i in range(16):
+            row, shift = divmod(i * width, LANES)
+            x = jnp.concatenate([norm_all[i % 8 * n_rows + 2 * g + i // 8] for g in range(8)], axis=0)
+            x = pltpu.roll(x, shift, 1) if shift else x
+            first = (spot >= shift) & (spot < shift + width)
+            parts[row] = jnp.where(first, x, parts[row])
+            if shift + width > LANES:
+                parts[row + 1] = jnp.where(spot < shift + width - LANES, x, parts[row + 1])
+        for g in range(8):
+            for row in range(5):
+                norm_lines[5 * g + row : 5 * g + row + 1, :] = parts[row][g : g + 1, :]
+        norm_line[...] = norm_lines[...].astype(jnp.bfloat16)
+
+    def norm_step(half):
+        for q in range(2):
+            @pl.when((half > 0) & (half <= reach[q]))
+            def _():
+                norm_turn(q, half).wait()
+
+            @pl.when(half < reach[q])
+            def _():
+                norm_turn(q, half + 1).start()
+
+        @pl.when(gateway & (half == meet))
+        def _():
+            norm_twin.start()
+
+        @pl.when(gateway & (half == meet + 1))
         def _():
             norm_twin.wait()
             norm_up.start()
             norm_down.start()
 
-        @pl.when(hop == 2)
+        @pl.when(gateway & (half == meet + 2))
         def _():
             norm_up.wait()
             norm_down.wait()
             norm_far.start()
 
-        @pl.when(hop == 3)
+        @pl.when(gateway & (half == meet + 3))
         def _():
             norm_far.wait()
-
-        turn_hop = hop - 2
+            assemble()
+
         for q in range(2):
-            @pl.when((turn_hop > 1) & (turn_hop <= reach[q] + 1))
+            @pl.when(half == meet + 4 + far[q])
             def _():
-                norm_turn(q, turn_hop - 1).wait()
-
-            @pl.when((turn_hop > 0) & (turn_hop <= reach[q]))
-            def _():
-                norm_turn(q, turn_hop).start()
+                pl.when(takes[q])(lambda: norm_pass(q).wait_recv())
+                pl.when(passes[q])(lambda: norm_pass(q).start())
 
     small[0].wait()
     low = low_buf[...].T
@@ -164,7 +200,7 @@
         loads[c].wait()
         mine_ref[c] = (train_buf[c].astype(jnp.float32) + mix_rate * delta).astype(jnp.bfloat16)
         if c == order[1]:
-            pl.semaphore_wait(barrier, 7)
+            pl.semaphore_wait(barrier, jnp.where(gateway, 7, 4))
         if before is not None:
             ring_copy(before, me, after[before // per_ring], 0, True).start()
         before = c
@@ -176,10 +212,9 @@
 
     for c in order:
         turn(c, me, True)
-    norm_twin.start()
 
     def arrived(hop, forward):
-        for c in order:
+        for i, c in enumerate(order):
             q = c // per_ring
             origin = ring_device(q // 2, (pos[q] + (n_rows - way[q]) * hop) % n_rows)
             ring_copy(c, origin, after[q], hop - 1).wait_recv()
@@ -187,27 +222,18 @@
             if forward:
                 ring_copy(c, origin, after[q], hop).start()
             turn(c, origin)
+            if forward and (i + 1) % (chunks // 2) == 0:
+                norm_step(2 * (hop - 1) + (i + 1) // (chunks // 2) - 1)
 
     def body(hop, carry):
         arrived(hop, True)
-        norm_step(hop)
         return carry
 
     lax.fori_loop(1, steps, body, 0)
 
-    parts = [jnp.zeros((8, LANES), jnp.float32) for _ in range(6)]
-    spot = lax.broadcasted_iota(jnp.int32, (8, LANES), 1)
-    for i in range(16):
-        row, shift = divmod(i * width, LANES)
-        x = jnp.concatenate([norm_all[16 * g + i] for g in range(8)], axis=0)
-        x = pltpu.roll(x, shift, 1) if shift else x
-        first = (spot >= shift) & (spot < shift + width)
-        parts[row] = jnp.where(first, x, parts[row])
-        if shift + width > LANES:
-            parts[row + 1] = jnp.where(spot < shift + width - LANES, x, parts[row + 1])
-    for g in range(8):
-        for row in range(5):
-            norm_out_ref[5 * g + row : 5 * g + row + 1, :] = parts[row][g : g + 1, :]
+    for q in range(2):
+        pl.when(passes[q])(lambda: norm_pass(q).wait_send())
+    norm_out_ref[...] = norm_line[...]
     arrived(steps, False)
 
 
@@ -216,7 +242,7 @@
     pl.run_scoped(
         functools.partial(kernel, n_rows, n_tp, depth, chunks, per_ring, *refs),
         sem((4,)), sem((chunks,)), sem((chunks,)), sem((n_rows - 1, chunks)),
-        sem((4,)), sem((4,)), sem((2, n_rows // 2)), sem((2, n_rows // 2)),
+        sem((4,)), sem((4,)), sem((2, n_rows // 2)), sem((2, n_rows // 2)), sem((2,)), sem((2,)),
     )
 
 
@@ -304,15 +330,14 @@
     )
 
 
-def write_kernel(pieces, held_ref, norm_ref, out_ref, norm_out_ref, norm_buf, sems):
+def write_kernel(pieces, held_ref, norm_ref, out_ref, norm_out_ref, sems):
     rows = held_ref.shape[0] // pieces
     copies = []
     for i in range(pieces):
         part = pl.ds(i * rows, rows)
         copies.append(pltpu.make_async_copy(held_ref.at[part, :], out_ref.at[part, :], sems.at[i]))
         copies[-1].start()
-    norm_buf[...] = norm_ref[...].astype(jnp.bfloat16)
-    copies.append(pltpu.make_async_copy(norm_buf, norm_out_ref, sems.at[pieces]))
+    copies.append(pltpu.make_async_copy(norm_ref, norm_out_ref, sems.at[pieces]))
     copies[-1].start()
     for copy in copies:
         copy.wait()
@@ -356,7 +381,7 @@
         out_shape=(
             pltpu.VMEM((width, n_rows * depth), jnp.bfloat16),
             pltpu.VMEM((chunks, depth, LANES), jnp.bfloat16),
-            pltpu.VMEM(norm_shape, jnp.float32),
+            pltpu.VMEM(norm_shape, jnp.bfloat16),
         ),
         in_specs=[anywhere] * 5,
         out_specs=(vmem, vmem, vmem),
@@ -367,6 +392,8 @@
             pltpu.VMEM((2, 1, own), jnp.float32),
             pltpu.VMEM((chunks, n_rows * depth, LANES), jnp.bfloat16),
             pltpu.VMEM((n_rows * n_tp, 1, LANES), jnp.float32),
+            pltpu.VMEM(norm_shape, jnp.float32),
+            pltpu.VMEM(norm_shape, jnp.bfloat16),
         ],
         compiler_params=pltpu.CompilerParams(
             collective_id=0, has_side_effects=True, vmem_limit_bytes=30 * 1024 * 1024
@@ -379,9 +406,9 @@
             jax.ShapeDtypeStruct(held.shape, held.dtype),
             jax.ShapeDtypeStruct(norm_shape, jnp.bfloat16),
         ),
-        in_specs=[anywhere, vmem],
+        in_specs=[anywhere, anywhere],
         out_specs=(anywhere, anywhere),
-        scratch_shapes=[pltpu.VMEM(norm_shape, jnp.bfloat16), pltpu.SemaphoreType.DMA((pieces + 1,))],
+        scratch_shapes=[pltpu.SemaphoreType.DMA((pieces + 1,))],
         compiler_params=pltpu.CompilerParams(vmem_limit_bytes=1024 * 1024),
     )(held, norm)
     patch = pl.pallas_call(

time: 145 us -> 143 us (0.986)
  Pallas kernels: 145 us -> 142 us
    pallas_call x1, Pallas kernels: 114 us -> 112 us  [per_device(): pl.pallas_call(functools.partial(scoped_kernel, n_rows, n_tp, depth, chun...]
where the time goes in v6:
time: 143 us
  Pallas kernels  142 us (99%)
    pallas_call x1, Pallas kernels, per_device(): pl.pallas_call(functools.partial(scoped_kernel, n_rows, n_tp, depth, chun...  112 us
    pallas_call x1, Pallas kernels, per_device(): pl.pallas_call(functools.partial(scoped_late_kernel, n_rows, depth, chunk...  18.4 us
    pallas_call x1, Pallas kernels, per_device(): pl.pallas_call(functools.partial(write_kernel, pieces), out_shape=(jax.Sh...  8.85 us

profile of v6, /device:TPU:1, one launch (start us, length us, event | category | flops | bytes accessed | tf_op | source)
XLA Modules:
  0.0 142.7 jit_solution(10495374599564779569)
XLA Ops:
  0.6 112.2 %shard_map.68 = (bf16[2560,5120]{1,0:T(8,128)(2,1)S(1)}, bf16[20,320,128]{2,1,0:T(8,128)(2,1)S(1)}, bf16[40,128]{1,0:T(8,128)(2,1)S(1)}) custom-call(bf16[320,2560]{1,0:T(8,128)(2,1)} %refs_0_.1, bf16[16,320]{1,0:T(8,128)(2,1)} %bitcast.4, bf16[16,2560]{1,0:T(8,128)(2,1)} %refs_2_.1, f32[1,40]{1,0:T(1,128)} %bitcast.5, f32[1,40]{1,0:T(1,128)} %bitcast.6), custom_call_target="tpu_custom_call" | custom-call | tf_op jit(solution)/shard_map/pallas_call | solution.py:379
  112.8 8.8 %shard_map.69 = (bf16[2560,5120]{1,0:T(8,128)(2,1)}, bf16[40,128]{1,0:T(8,128)(2,1)}) custom-call(bf16[2560,5120]{1,0:T(8,128)(2,1)S(1)} %get-tuple-element.7.held_ref, bf16[40,128]{1,0:T(8,128)(2,1)S(1)} %get-tuple-element.8.norm_ref), custom_call_target="tpu_custom_call" | custom-call | tf_op jit(solution)/shard_map/pallas_call | solution.py:403
  121.7 18.4 %shard_map.70.patch_ref = bf16[3,2560,384]{2,1,0:T(8,128)(2,1)S(1)} custom-call(bf16[2560,5120]{1,0:T(8,128)(2,1)} %get-tuple-element.9.refs_0_.first_ref, bf16[20,320,128]{2,1,0:T(8,128)(2,1)S(1)} %get-tuple-element.10.refs_1_), custom_call_target="tpu_custom_call" | custom-call | tf_op jit(solution)/shard_map/pallas_call | solution.py:414
  140.1 2.7 %shard_map.71 = bf16[2560,5120]{1,0:T(8,128)(2,1)} custom-call(bf16[3,2560,384]{2,1,0:T(8,128)(2,1)S(1)} %shard_map.70.patch_ref, bf16[2560,5120]{1,0:T(8,128)(2,1)} %get-tuple-element.9.refs_0_.first_ref), custom_call_target="tpu_custom_call", output_to_operand_aliasing={{}: (1, {})} | custom-call | tf_op jit(solution)/shard_map/pallas_call | solution.py:427

commit v7 on v6

--- a/solution.py
+++ b/solution.py
@@ -9,7 +9,7 @@
 
 mix_rate = 2.0
 MESH = pl.DeviceIdType.MESH
-SPLIT = 3
+SPLIT = 4
 SIDE = 4
 LANES = 128
 
@@ -36,7 +36,7 @@
 
 
 def splits(tp):
-    return tp % 2
+    return 1 + (SPLIT - 1) * (tp % 2)
 
 
 def kernel(
@@ -48,7 +48,7 @@
 ):
     me = lax.axis_index("rows")
     my_tp = lax.axis_index("tp")
-    steps = n_rows - 1 - SPLIT * splits(my_tp)
+    steps = n_rows - 1 - splits(my_tp)
     pos = [ring_position(q // 2, me) for q in range(4)]
     way = [1 if q % 2 == 0 else n_rows - 1 for q in range(4)]
     after = [ring_device(q // 2, (pos[q] + way[q]) % n_rows) for q in range(4)]
@@ -230,6 +230,7 @@
         return carry
 
     lax.fori_loop(1, steps, body, 0)
+    norm_step(2 * (steps - 1))
 
     for q in range(2):
         pl.when(passes[q])(lambda: norm_pass(q).wait_send())
@@ -259,6 +260,7 @@
 ):
     me = lax.axis_index("rows")
     my_tp = lax.axis_index("tp")
+    count = splits(my_tp)
     order = [q * per_ring + k for k in range(per_ring) for q in range(4)]
 
     def neighbour(q, step):
@@ -293,7 +295,7 @@
         shared = patch_ref.at[slot, rows, 256:384]
         put_half(shared, jnp.concatenate([rest, rest], axis=0).T, odd)
 
-        @pl.when((gap == 0) | (gap > SPLIT))
+        @pl.when((gap == 0) | (gap > count))
         def _():
             put_half(shared, stash[slot, rows, :], 1 - odd)
 
@@ -301,24 +303,29 @@
         def _():
             put_half(shared, patch_ref[gap - 1, rows, 256:384], 1 - odd)
 
-    @pl.when(splits(my_tp) == 1)
-    def _():
-        barrier = pltpu.get_barrier_semaphore()
-        for q in range(4):
-            pl.semaphore_signal(barrier, inc=1, device_id=(neighbour(q, 1), my_tp), device_id_type=MESH)
-        pl.semaphore_wait(barrier, 4)
-        for c in order:
-            late_copy(c, 0, True).start()
-        stashed = [stash_copy(q, slot) for slot in range(SPLIT) for q in range(4)]
-        for copy in stashed:
-            copy.start()
-        for copy in stashed:
-            copy.wait()
-        for hop in range(SPLIT):
+    barrier = pltpu.get_barrier_semaphore()
+    for q in range(4):
+        pl.semaphore_signal(barrier, inc=1, device_id=(neighbour(q, 1), my_tp), device_id_type=MESH)
+    pl.semaphore_wait(barrier, 4)
+    for c in order:
+        late_copy(c, 0, True).start()
+    for slot in range(SPLIT):
+        @pl.when(slot < count)
+        def _():
+            for q in range(4):
+                stash_copy(q, slot).start()
+    for slot in range(SPLIT):
+        @pl.when(slot < count)
+        def _():
+            for q in range(4):
+                stash_copy(q, slot).wait()
+    for hop in range(SPLIT):
+        @pl.when(hop < count)
+        def _():
             for c in order:
                 late_copy(c, hop, hop == 0).wait()
                 if hop + 1 < SPLIT:
-                    late_copy(c, hop + 1, False).start()
+                    pl.when(hop + 1 < count)(lambda: late_copy(c, hop + 1, False).start())
                 turn(c, hop)
 
 
@@ -345,6 +352,7 @@
 
 def patch_kernel(n_rows, depth, quarter, patch_ref, first_ref, out_ref, main_sem, shared_sem):
     me = lax.axis_index("rows")
+    count = splits(lax.axis_index("tp"))
 
     def copies(q, slot):
         origin, gap = late_place(n_rows, q, me, slot + 1)
@@ -355,17 +363,20 @@
         main = pltpu.make_async_copy(patch_ref.at[slot, rows, 0:256], out_ref.at[rows, lanes], main_sem.at[slot, q])
         shared = pltpu.make_async_copy(
             patch_ref.at[slot, rows, 256:384], out_ref.at[rows, shared_lanes], shared_sem.at[slot, q])
-        return main, shared, (gap <= slot) | (gap > SPLIT)
-
-    @pl.when(splits(lax.axis_index("tp")) == 1)
-    def _():
-        everything = [copies(q, slot) for slot in range(SPLIT) for q in range(4)]
-        for main, shared, last in everything:
-            main.start()
-            pl.when(last)(shared.start)
-        for main, shared, last in everything:
-            main.wait()
-            pl.when(last)(shared.wait)
+        return main, shared, (gap <= slot) | (gap > count)
+
+    for slot in range(SPLIT):
+        @pl.when(slot < count)
+        def _():
+            for main, shared, last in [copies(q, slot) for q in range(4)]:
+                main.start()
+                pl.when(last)(shared.start)
+    for slot in range(SPLIT):
+        @pl.when(slot < count)
+        def _():
+            for main, shared, last in [copies(q, slot) for q in range(4)]:
+                main.wait()
+                pl.when(last)(shared.wait)
 
 
 def per_device(train_up, low_up, high_up, norm_train, norm_step):

time: 143 us -> 142 us (level)
  Pallas kernels: 142 us -> 140 us
    pallas_call x1, Pallas kernels: 112 us -> 103 us  [per_device(): pl.pallas_call(functools.partial(scoped_kernel, n_rows, n_tp, depth, chun...]
    pallas_call x1, Pallas kernels: 18.4 us -> 24.9 us  [per_device(): pl.pallas_call(functools.partial(scoped_late_kernel, n_rows, depth, chunk...]
where the time goes in v7:
time: 142 us; the launch traced here: 141 us
  Pallas kernels  140 us (99%)
    pallas_call x1, Pallas kernels, per_device(): pl.pallas_call(functools.partial(scoped_kernel, n_rows, n_tp, depth, chun...  103 us
    pallas_call x1, Pallas kernels, per_device(): pl.pallas_call(functools.partial(scoped_late_kernel, n_rows, depth, chunk...  24.9 us
    pallas_call x1, Pallas kernels, per_device(): pl.pallas_call(functools.partial(write_kernel, pieces), out_shape=(jax.Sh...  8.85 us
    pallas_call x1, Pallas kernels, per_device(): pl.pallas_call(functools.partial(patch_kernel, n_rows, depth, width // 4)...  3.25 us

profile of v7, /device:TPU:1, one launch (start us, length us, event | category | flops | bytes accessed | tf_op | source)
XLA Modules:
  0.0 141.2 jit_solution(13178330900284689874)
XLA Ops:
  0.6 103.4 %shard_map.68 = (bf16[2560,5120]{1,0:T(8,128)(2,1)S(1)}, bf16[20,320,128]{2,1,0:T(8,128)(2,1)S(1)}, bf16[40,128]{1,0:T(8,128)(2,1)S(1)}) custom-call(bf16[320,2560]{1,0:T(8,128)(2,1)} %refs_0_.1, bf16[16,320]{1,0:T(8,128)(2,1)} %bitcast.4, bf16[16,2560]{1,0:T(8,128)(2,1)} %refs_2_.1, f32[1,40]{1,0:T(1,128)} %bitcast.5, f32[1,40]{1,0:T(1,128)} %bitcast.6), custom_call_target="tpu_custom_call" | custom-call | tf_op jit(solution)/shard_map/pallas_call | solution.py:390
  104.0 8.8 %shard_map.69 = (bf16[2560,5120]{1,0:T(8,128)(2,1)}, bf16[40,128]{1,0:T(8,128)(2,1)}) custom-call(bf16[2560,5120]{1,0:T(8,128)(2,1)S(1)} %get-tuple-element.7.held_ref, bf16[40,128]{1,0:T(8,128)(2,1)S(1)} %get-tuple-element.8.norm_ref), custom_call_target="tpu_custom_call" | custom-call | tf_op jit(solution)/shard_map/pallas_call | solution.py:414
  112.9 24.9 %shard_map.70.patch_ref = bf16[4,2560,384]{2,1,0:T(8,128)(2,1)S(1)} custom-call(bf16[2560,5120]{1,0:T(8,128)(2,1)} %get-tuple-element.9.refs_0_.first_ref, bf16[20,320,128]{2,1,0:T(8,128)(2,1)S(1)} %get-tuple-element.10.refs_1_), custom_call_target="tpu_custom_call" | custom-call | tf_op jit(solution)/shard_map/pallas_call | solution.py:425
  137.8 3.2 %shard_map.71 = bf16[2560,5120]{1,0:T(8,128)(2,1)} custom-call(bf16[4,2560,384]{2,1,0:T(8,128)(2,1)S(1)} %shard_map.70.patch_ref, bf16[2560,5120]{1,0:T(8,128)(2,1)} %get-tuple-element.9.refs_0_.first_ref), custom_call_target="tpu_custom_call", output_to_operand_aliasing={{}: (1, {})} | custom-call | tf_op jit(solution)/shard_map/pallas_call | solution.py:438

commit v8 on v7

--- a/solution.py
+++ b/solution.py
@@ -208,10 +208,11 @@
     small[3].wait()
     norm_all[slot, :, :] = jnp.zeros((1, LANES), jnp.float32)
     norm_all[slot, :, 0:width] = norm_buf[0] + norm_buf[1]
-    ring_copy(before, me, after[before // per_ring], 0, True).start()
-
-    for c in order:
+
+    for i, c in enumerate(order):
         turn(c, me, True)
+        if i == 0:
+            ring_copy(before, me, after[before // per_ring], 0, True).start()
 
     def arrived(hop, forward):
         for i, c in enumerate(order):

time: 142 us -> 142 us (level)
  no operation moved by 1% of the time
where the time goes in v8:
time: 142 us; the launch traced here: 141 us
  Pallas kernels  140 us (99%)
    pallas_call x1, Pallas kernels, per_device(): pl.pallas_call(functools.partial(scoped_kernel, n_rows, n_tp, depth, chun...  103 us
    pallas_call x1, Pallas kernels, per_device(): pl.pallas_call(functools.partial(scoped_late_kernel, n_rows, depth, chunk...  24.9 us
    pallas_call x1, Pallas kernels, per_device(): pl.pallas_call(functools.partial(write_kernel, pieces), out_shape=(jax.Sh...  8.85 us
    pallas_call x1, Pallas kernels, per_device(): pl.pallas_call(functools.partial(patch_kernel, n_rows, depth, width // 4)...  3.25 us

profile of v8, /device:TPU:1, one launch (start us, length us, event | category | flops | bytes accessed | tf_op | source)
XLA Modules:
  0.0 141.2 jit_solution(10643766000210604646)
XLA Ops:
  0.6 103.4 %shard_map.68 = (bf16[2560,5120]{1,0:T(8,128)(2,1)S(1)}, bf16[20,320,128]{2,1,0:T(8,128)(2,1)S(1)}, bf16[40,128]{1,0:T(8,128)(2,1)S(1)}) custom-call(bf16[320,2560]{1,0:T(8,128)(2,1)} %refs_0_.1, bf16[16,320]{1,0:T(8,128)(2,1)} %bitcast.4, bf16[16,2560]{1,0:T(8,128)(2,1)} %refs_2_.1, f32[1,40]{1,0:T(1,128)} %bitcast.5, f32[1,40]{1,0:T(1,128)} %bitcast.6), custom_call_target="tpu_custom_call" | custom-call | tf_op jit(solution)/shard_map/pallas_call | solution.py:391
  104.0 8.8 %shard_map.69 = (bf16[2560,5120]{1,0:T(8,128)(2,1)}, bf16[40,128]{1,0:T(8,128)(2,1)}) custom-call(bf16[2560,5120]{1,0:T(8,128)(2,1)S(1)} %get-tuple-element.7.held_ref, bf16[40,128]{1,0:T(8,128)(2,1)S(1)} %get-tuple-element.8.norm_ref), custom_call_target="tpu_custom_call" | custom-call | tf_op jit(solution)/shard_map/pallas_call | solution.py:415
  112.9 24.9 %shard_map.70.patch_ref = bf16[4,2560,384]{2,1,0:T(8,128)(2,1)S(1)} custom-call(bf16[2560,5120]{1,0:T(8,128)(2,1)} %get-tuple-element.9.refs_0_.first_ref, bf16[20,320,128]{2,1,0:T(8,128)(2,1)S(1)} %get-tuple-element.10.refs_1_), custom_call_target="tpu_custom_call" | custom-call | tf_op jit(solution)/shard_map/pallas_call | solution.py:426
  137.8 3.2 %shard_map.71 = bf16[2560,5120]{1,0:T(8,128)(2,1)} custom-call(bf16[4,2560,384]{2,1,0:T(8,128)(2,1)S(1)} %shard_map.70.patch_ref, bf16[2560,5120]{1,0:T(8,128)(2,1)} %get-tuple-element.9.refs_0_.first_ref), custom_call_target="tpu_custom_call", output_to_operand_aliasing={{}: (1, {})} | custom-call | tf_op jit(solution)/shard_map/pallas_call | solution.py:439

commit v9 on v8

--- a/solution.py
+++ b/solution.py
@@ -291,9 +291,9 @@
         odd = origin % 2
         rows = pl.ds(c * LANES, LANES)
         main = late[slot, c, pl.ds(pl.multiple_of(odd * 64, 64), 256), :]
-        patch_ref[slot, rows, 0:256] = main.T
+        patch_ref[slot, rows, pl.ds(pl.multiple_of(odd * LANES, LANES), 256)] = main.T
         rest = late[slot, c, pl.ds(pl.multiple_of((1 - odd) * 256, 64), 64), :]
-        shared = patch_ref.at[slot, rows, 256:384]
+        shared = patch_ref.at[slot, rows, pl.ds(pl.multiple_of((1 - odd) * 256, LANES), LANES)]
         put_half(shared, jnp.concatenate([rest, rest], axis=0).T, odd)
 
         @pl.when((gap == 0) | (gap > count))
@@ -302,7 +302,7 @@
 
         @pl.when((gap > 0) & (gap <= slot))
         def _():
-            put_half(shared, patch_ref[gap - 1, rows, 256:384], 1 - odd)
+            put_half(shared, patch_ref[gap - 1, rows, pl.ds(pl.multiple_of(odd * 256, LANES), LANES)], 1 - odd)
 
     barrier = pltpu.get_barrier_semaphore()
     for q in range(4):
@@ -351,33 +351,37 @@
         copy.wait()
 
 
-def patch_kernel(n_rows, depth, quarter, patch_ref, first_ref, out_ref, main_sem, shared_sem):
+def patch_kernel(n_rows, depth, quarter, patch_ref, first_ref, out_ref, sems):
     me = lax.axis_index("rows")
     count = splits(lax.axis_index("tp"))
 
-    def copies(q, slot):
-        origin, gap = late_place(n_rows, q, me, slot + 1)
-        base = origin // 2 * 2 * depth
-        rows = pl.ds(q * quarter, quarter)
-        lanes = pl.ds(pl.multiple_of(base + origin % 2 * 384, LANES), 256)
-        shared_lanes = pl.ds(pl.multiple_of(base + 256, LANES), LANES)
-        main = pltpu.make_async_copy(patch_ref.at[slot, rows, 0:256], out_ref.at[rows, lanes], main_sem.at[slot, q])
-        shared = pltpu.make_async_copy(
-            patch_ref.at[slot, rows, 256:384], out_ref.at[rows, shared_lanes], shared_sem.at[slot, q])
-        return main, shared, (gap <= slot) | (gap > count)
-
-    for slot in range(SPLIT):
-        @pl.when(slot < count)
-        def _():
-            for main, shared, last in [copies(q, slot) for q in range(4)]:
-                main.start()
-                pl.when(last)(shared.start)
-    for slot in range(SPLIT):
-        @pl.when(slot < count)
-        def _():
-            for main, shared, last in [copies(q, slot) for q in range(4)]:
-                main.wait()
-                pl.when(last)(shared.wait)
+    def each(act):
+        for slot in range(SPLIT):
+            @pl.when(slot < count)
+            def _():
+                for q in range(4):
+                    origin, gap = late_place(n_rows, q, me, slot + 1)
+                    odd = origin % 2
+                    base = origin // 2 * 2 * depth
+                    rows = pl.ds(q * quarter, quarter)
+                    last = (gap <= slot) | (gap > count)
+
+                    def copy(start, to, lanes):
+                        return pltpu.make_async_copy(
+                            patch_ref.at[slot, rows, pl.ds(start, lanes)],
+                            out_ref.at[rows, pl.ds(pl.multiple_of(to, LANES), lanes)],
+                            sems.at[slot, q])
+
+                    @pl.when(last)
+                    def _():
+                        act(copy(0, base + odd * 256, 384))
+
+                    @pl.when(jnp.logical_not(last))
+                    def _():
+                        act(copy(pl.multiple_of(odd * LANES, LANES), base + odd * 384, 256))
+
+    each(lambda copy: copy.start())
+    each(lambda copy: copy.wait())
 
 
 def per_device(train_up, low_up, high_up, norm_train, norm_step):
@@ -442,7 +446,7 @@
         in_specs=[anywhere, anywhere],
         out_specs=anywhere,
         input_output_aliases={1: 0},
-        scratch_shapes=[pltpu.SemaphoreType.DMA((SPLIT, 4)), pltpu.SemaphoreType.DMA((SPLIT, 4))],
+        scratch_shapes=[pltpu.SemaphoreType.DMA((SPLIT, 4))],
         compiler_params=pltpu.CompilerParams(vmem_limit_bytes=1024 * 1024),
     )(patch, first)
     return ready, norm.reshape(-1)

time: 142 us -> 141 us (level)
  no operation moved by 1% of the time
where the time goes in v9:
time: 141 us
  Pallas kernels  140 us (99%)
    pallas_call x1, Pallas kernels, per_device(): pl.pallas_call(functools.partial(scoped_kernel, n_rows, n_tp, depth, chun...  103 us
    pallas_call x1, Pallas kernels, per_device(): pl.pallas_call(functools.partial(scoped_late_kernel, n_rows, depth, chunk...  24.9 us
    pallas_call x1, Pallas kernels, per_device(): pl.pallas_call(functools.partial(write_kernel, pieces), out_shape=(jax.Sh...  8.85 us
    pallas_call x1, Pallas kernels, per_device(): pl.pallas_call(functools.partial(patch_kernel, n_rows, depth, width // 4)...  3.13 us

profile of v9, /device:TPU:1, one launch (start us, length us, event | category | flops | bytes accessed | tf_op | source)
XLA Modules:
  0.0 141.1 jit_solution(12987811747921157341)
XLA Ops:
  0.6 103.4 %shard_map.68 = (bf16[2560,5120]{1,0:T(8,128)(2,1)S(1)}, bf16[20,320,128]{2,1,0:T(8,128)(2,1)S(1)}, bf16[40,128]{1,0:T(8,128)(2,1)S(1)}) custom-call(bf16[320,2560]{1,0:T(8,128)(2,1)} %refs_0_.1, bf16[16,320]{1,0:T(8,128)(2,1)} %bitcast.4, bf16[16,2560]{1,0:T(8,128)(2,1)} %refs_2_.1, f32[1,40]{1,0:T(1,128)} %bitcast.5, f32[1,40]{1,0:T(1,128)} %bitcast.6), custom_call_target="tpu_custom_call" | custom-call | tf_op jit(solution)/shard_map/pallas_call | solution.py:395
  104.0 8.8 %shard_map.69 = (bf16[2560,5120]{1,0:T(8,128)(2,1)}, bf16[40,128]{1,0:T(8,128)(2,1)}) custom-call(bf16[2560,5120]{1,0:T(8,128)(2,1)S(1)} %get-tuple-element.7.held_ref, bf16[40,128]{1,0:T(8,128)(2,1)S(1)} %get-tuple-element.8.norm_ref), custom_call_target="tpu_custom_call" | custom-call | tf_op jit(solution)/shard_map/pallas_call | solution.py:419
  112.9 24.9 %shard_map.70.patch_ref = bf16[4,2560,384]{2,1,0:T(8,128)(2,1)S(1)} custom-call(bf16[2560,5120]{1,0:T(8,128)(2,1)} %get-tuple-element.9.refs_0_.first_ref, bf16[20,320,128]{2,1,0:T(8,128)(2,1)S(1)} %get-tuple-element.10.refs_1_), custom_call_target="tpu_custom_call" | custom-call | tf_op jit(solution)/shard_map/pallas_call | solution.py:430
  137.8 3.1 %shard_map.71 = bf16[2560,5120]{1,0:T(8,128)(2,1)} custom-call(bf16[4,2560,384]{2,1,0:T(8,128)(2,1)S(1)} %shard_map.70.patch_ref, bf16[2560,5120]{1,0:T(8,128)(2,1)} %get-tuple-element.9.refs_0_.first_ref), custom_call_target="tpu_custom_call", output_to_operand_aliasing={{}: (1, {})} | custom-call | tf_op jit(solution)/shard_map/pallas_call | solution.py:443
